TPU v7x, 32 devices: a whole 2x2x4 slice. The times are simulated.
32 devices in a mesh: mc: 8 (over z, x), mr: 4 (over y, core).
Axes of the slice: x: 2, y: 2, z: 4, core: 2. Of those that a mesh axis runs over, the one named last changes fastest.
Arguments:
- column_panel: float32 [4096, 256], P('mc', 'mr'), may hold values from -0.375 to 0.375
- diag_block: float32 [256, 256], P('mc', 'mr'), may hold values from -4.3 to 4.3, as said below
- row_panel: float32 [256, 32768], P('mc', 'mr'), may hold values from -6 to 6
- trailing: float32 [4096, 32768], P('mc', 'mr'), may hold values from -6 to 6
Outputs:
- solved_panel: float32 [4096, 256], P('mc', 'mr')
- inverse_block: float32 [256, 256], P('mc', 'mr')
- scaled_panel: float32 [256, 32768], P('mc', 'mr')
- updated: float32 [4096, 32768], P('mc', 'mr')
Inputs may be any that keep to these rules, and one draw needn't show every extreme that they name: `diag_block`: upper triangle with a diagonal of magnitude 2 to 4 and small off-diagonal entries.
All inputs are finite; a program needn't handle non-finite values.
Results may differ from a plain program's by a relative error of at most 0.00011.
Values sent between devices are 32-bit elements; how exact they have to be, the bound alone decides.
A program may use at most 128 MiB of HBM per device.

v0:
```python
import functools

import jax
import jax.numpy as jnp
from jax import lax
from jax.experimental import pallas as pl
from jax.experimental.pallas import tpu as pltpu
from jax.sharding import PartitionSpec as P

VMEM_BYTES = 67043328
HIGHEST = lax.Precision.HIGHEST


def dot(a, b):
    return jnp.dot(a, b, precision=HIGHEST, preferred_element_type=jnp.float32)


def upper_inverse(matrix):
    order = matrix.shape[0]
    row = lax.broadcasted_iota(jnp.int32, (order, order), 0)
    col = lax.broadcasted_iota(jnp.int32, (order, order), 1)
    on_diag = row == col
    pivots = jnp.where(on_diag, matrix, 0.0)
    recip_col = 1.0 / jnp.sum(pivots, axis=1, keepdims=True)
    recip_row = 1.0 / jnp.sum(pivots, axis=0, keepdims=True)
    power = -(recip_col * jnp.where(col > row, matrix, 0.0))
    identity = jnp.where(on_diag, 1.0, 0.0)
    product = identity + power
    steps = max((order - 1).bit_length(), 1)
    for level in range(steps - 1):
        power = dot(power, power)
        product = dot(product, identity + power)
    return product * recip_row


def split(value):
    high = value.astype(jnp.bfloat16)
    low = (value - high.astype(jnp.float32)).astype(jnp.bfloat16)
    return high, low


def kernel(n_mc, n_mr, chunks, tile,
           column_ref, diag_ref, row_ref, trailing_ref,
           solved_ref, inverse_ref, scaled_ref, updated_ref,
           panel, columns, diags, matrix, flipped, left_high, left_low,
           load_sem, trail_sem, send_sem, recv_sem,
           diag_send, diag_recv, block_send, block_recv, col_send, col_recv):
    mc = lax.axis_index("mc")
    mr = lax.axis_index("mr")
    levels = n_mc // 2
    z = mc // 2
    x = lax.rem(mc, 2)
    rows = row_ref.shape[0]
    half = rows // 2
    cols = row_ref.shape[1]
    width = cols // chunks
    block_cols = diag_ref.shape[1]
    height = column_ref.shape[1]

    def at(mc_index, mr_index):
        return {"mc": mc_index, "mr": mr_index}

    own_row = pltpu.make_async_copy(
        row_ref, panel.at[pl.ds(pl.multiple_of(mc * rows, rows), rows)], load_sem.at[0])
    own_diag = pltpu.make_async_copy(
        diag_ref, diags.at[mr, pl.ds(pl.multiple_of(mc * rows, rows), rows)], load_sem.at[1])
    own_part = lambda k: pl.ds(pl.multiple_of(k * block_cols, block_cols), block_cols)
    own_column = pltpu.make_async_copy(column_ref, columns.at[own_part(mr)], load_sem.at[2])
    own_row.start()
    own_diag.start()
    own_column.start()

    barrier = pltpu.get_barrier_semaphore()
    for step in range(1, n_mc):
        pl.semaphore_signal(barrier, inc=1, device_id=at(lax.rem(mc + step, n_mc), mr),
                            device_id_type=pl.DeviceIdType.MESH)
    for step in range(1, n_mr):
        pl.semaphore_signal(barrier, inc=1, device_id=at(mc, lax.rem(mr + step, n_mr)),
                            device_id_type=pl.DeviceIdType.MESH)
    pl.semaphore_wait(barrier, n_mc + n_mr - 2)

    def piece(shard, c, low=None):
        first = pl.multiple_of(shard * rows, rows)
        count = rows
        if low is not None:
            first = pl.multiple_of(shard * rows + low * half, half)
            count = half
        return panel.at[pl.ds(first, count), pl.ds(pl.multiple_of(c * width, width), width)]

    def copy(shard, c, way, slot, target, low=None):
        ref = piece(shard, c, low)
        return pltpu.make_async_remote_copy(
            src_ref=ref, dst_ref=ref,
            send_sem=send_sem.at[way, slot, c],
            recv_sem=recv_sem.at[2 * shard + (1 if low == 1 else 0), c],
            device_id=at(target, mr), device_id_type=pl.DeviceIdType.MESH)

    down = jnp.maximum(mc - 2, 0)
    up = jnp.minimum(mc + 2, n_mc - 1)
    across = z * 2 + 1 - x

    def diag_copy(step, source, target):
        ref = diags.at[mr, pl.ds(pl.multiple_of(source * rows, rows), rows)]
        return pltpu.make_async_remote_copy(
            src_ref=ref, dst_ref=ref, send_sem=diag_send.at[step], recv_sem=diag_recv.at[step],
            device_id=at(target, mr), device_id_type=pl.DeviceIdType.MESH)

    def block_copy(step, source, target):
        ref = diags.at[source]
        return pltpu.make_async_remote_copy(
            src_ref=ref, dst_ref=ref, send_sem=block_send.at[step], recv_sem=block_recv.at[step],
            device_id=at(mc, target), device_id_type=pl.DeviceIdType.MESH)

    def column_copy(step, source, target):
        ref = columns.at[own_part(source)]
        return pltpu.make_async_remote_copy(
            src_ref=ref, dst_ref=ref, send_sem=col_send.at[step], recv_sem=col_recv.at[step],
            device_id=at(mc, target), device_id_type=pl.DeviceIdType.MESH)

    own_row.wait()

    @pl.loop(0, chunks)
    def _(c):
        @pl.when(z > 0)
        def _():
            copy(mc, c, 0, z, down).start()

        @pl.when(z < levels - 1)
        def _():
            copy(mc, c, 1, z, up).start()

        copy(mc, c, 2, z, across).start()

    own_diag.wait()
    for step in range(1, n_mc):
        diag_copy(step, mc, lax.rem(mc + step, n_mc)).start()

    own_column.wait()
    for step in range(1, n_mr):
        column_copy(step, mr, lax.rem(mr + step, n_mr)).start()

    def trail_copy(c):
        part = pl.ds(pl.multiple_of(c * width, width), width)
        return pltpu.make_async_copy(trailing_ref.at[:, part], updated_ref.at[:, part], trail_sem.at[c])

    @pl.loop(0, chunks)
    def _(c):
        trail_copy(c).start()

    first_half_only = lambda q: jnp.logical_or(
        jnp.logical_and(q == levels - 1, z != levels - 1), jnp.logical_and(q == 0, z != 0))

    def each_across(q, c, act):
        @pl.when(first_half_only(q))
        def _():
            act(copy(2 * q + x, c, 2, q, across, 0))

        @pl.when(jnp.logical_not(first_half_only(q)))
        def _():
            act(copy(2 * q + x, c, 2, q, across))

    start = lambda d: d.start()
    other = 1 - x
    top = 2 * (levels - 1) + other
    bottom = other

    def invert():
        for step in range(1, n_mc):
            diag_copy(step, lax.rem(mc + n_mc - step, n_mc), lax.rem(mc + step, n_mc)).wait_recv()
        for step in range(1, n_mr):
            block_copy(step, mr, lax.rem(mr + step, n_mr)).start()
        for step in range(1, n_mr):
            block_copy(step, lax.rem(mr + n_mr - step, n_mr), lax.rem(mr + step, n_mr)).wait_recv()
        for k in range(n_mr):
            matrix[:, k * block_cols:(k + 1) * block_cols] = diags[k]
        matrix[...] = upper_inverse(matrix[...])
        own_inverse = matrix[pl.ds(pl.multiple_of(mc * rows, rows), rows), :]
        for step in range(1, n_mr):
            column_copy(step, lax.rem(mr + n_mr - step, n_mr), lax.rem(mr + step, n_mr)).wait_recv()
        flipped[...] = -lax.dot_general(
            matrix[...], columns[...], (((0,), (0,)), ((), ())),
            precision=HIGHEST, preferred_element_type=jnp.float32)
        solved_ref[...] = flipped[own_part(mr), :]
        left_high[0:height, :], left_low[0:height, :] = split(flipped[...].T)
        left_high[height:height + rows, :], left_low[height:height + rows, :] = split(own_inverse)
        for k in range(n_mr):
            @pl.when(mr == k)
            def _():
                inverse_ref[...] = own_inverse[:, k * block_cols:(k + 1) * block_cols]

    for phase in range(levels - 1):
        if phase == min(1, levels - 2):
            invert()

        above = z + 1 + phase
        below = z - 1 - phase

        @pl.loop(0, chunks)
        def _(c):
            @pl.when(above < levels)
            def _():
                copy(2 * above + x, c, 0, above, down).wait_recv()

                @pl.when(z > 0)
                def _():
                    copy(2 * above + x, c, 0, above, down).start()

                each_across(above, c, start)

            @pl.when(below >= 0)
            def _():
                copy(2 * below + x, c, 1, below, up).wait_recv()

                @pl.when(z < levels - 1)
                def _():
                    copy(2 * below + x, c, 1, below, up).start()

                each_across(below, c, start)

            if phase == 0:
                copy(2 * z + other, c, 2, z, across).wait_recv()

                @pl.when(z == levels - 1)
                def _():
                    copy(top, c, 0, levels, down, 1).start()

                @pl.when(z == 0)
                def _():
                    copy(bottom, c, 1, levels, up, 1).start()

            @pl.when(above == levels)
            def _():
                @pl.when(z < levels - 1)
                def _():
                    copy(top, c, 0, levels, down, 1).wait_recv()

                    @pl.when(z > 0)
                    def _():
                        copy(top, c, 0, levels, down, 1).start()

            @pl.when(below == -1)
            def _():
                @pl.when(z > 0)
                def _():
                    copy(bottom, c, 1, levels, up, 1).wait_recv()

                    @pl.when(z < levels - 1)
                    def _():
                        copy(bottom, c, 1, levels, up, 1).start()

    @pl.loop(0, chunks)
    def _(c):
        trail_copy(c).wait()

        @pl.when(z == 0)
        def _():
            copy(top, c, 0, levels, down, 1).wait_recv()

        @pl.when(z == levels - 1)
        def _():
            copy(bottom, c, 1, levels, up, 1).wait_recv()

        for q in range(levels):
            def receive(low):
                copy(2 * q + other, c, 2, q, across, low).wait_recv()

            @pl.when(jnp.logical_and(z != q, first_half_only(q)))
            def _():
                receive(0)

            @pl.when(jnp.logical_and(z != q, jnp.logical_not(first_half_only(q))))
            def _():
                receive(None)

        for t in range(width // tile):
            part = pl.ds(pl.multiple_of(c * width + t * tile, tile), tile)
            right_high, right_low = split(panel[:, part])
            product = jnp.dot(left_high[...], right_low, preferred_element_type=jnp.float32)
            product += jnp.dot(left_low[...], right_high, preferred_element_type=jnp.float32)
            product += jnp.dot(left_high[...], right_high, preferred_element_type=jnp.float32)
            updated_ref[:, part] = updated_ref[:, part] + product[0:height]
            scaled_ref[:, part] = product[height:height + rows]

    for step in range(1, n_mc):
        diag_copy(step, mc, lax.rem(mc + step, n_mc)).wait_send()
    for step in range(1, n_mr):
        block_copy(step, mr, lax.rem(mr + step, n_mr)).wait_send()
        column_copy(step, mr, lax.rem(mr + step, n_mr)).wait_send()

    @pl.loop(0, chunks)
    def _(c):
        for q in range(levels):
            @pl.when(jnp.logical_and(z > 0, z <= q))
            def _():
                copy(2 * q + x, c, 0, q, down).wait_send()

            @pl.when(jnp.logical_and(z < levels - 1, z >= q))
            def _():
                copy(2 * q + x, c, 1, q, up).wait_send()

            each_across(q, c, lambda d: d.wait_send())

        @pl.when(z > 0)
        def _():
            copy(top, c, 0, levels, down, 1).wait_send()

        @pl.when(z < levels - 1)
        def _():
            copy(bottom, c, 1, levels, up, 1).wait_send()


def store(*refs):
    sources, targets, sem = refs[:4], refs[4:8], refs[8]
    strips = sem.shape[0] - 3
    deep = sources[3].shape[0] // strips
    copies = []
    for i in range(strips):
        part = pl.ds(i * deep, deep)
        copies.append(pltpu.make_async_copy(sources[3].at[part], targets[3].at[part], sem.at[3 + i]))
    for i in range(3):
        copies.append(pltpu.make_async_copy(sources[i], targets[i], sem.at[i]))
    for c in copies:
        c.start()
    for c in copies:
        c.wait()


def shards(n_mc, n_mr, column_panel, diag_block, row_panel, trailing):
    rows, block_cols = diag_block.shape
    height, cols = trailing.shape
    order = rows * n_mc
    levels = n_mc // 2
    chunks = max(1, 16 // levels)
    while cols % (chunks * 128):
        chunks //= 2
    width = cols // chunks
    tile = 512 if width % 512 == 0 else 128
    held = 4 * (height * cols + rows * cols + block_cols * height + rows * 128) + 64 * 1024
    dma = pltpu.SemaphoreType.DMA
    f32 = jnp.float32
    anywhere = pl.BlockSpec(memory_space=pl.ANY)
    vmem = pl.BlockSpec(memory_space=pltpu.VMEM)
    parts = pl.pallas_call(
        functools.partial(kernel, n_mc, n_mr, chunks, tile),
        out_shape=(
            pltpu.VMEM((block_cols, height), f32),
            pltpu.VMEM(diag_block.shape, f32),
            pltpu.VMEM(row_panel.shape, f32),
            pltpu.VMEM(trailing.shape, f32),
        ),
        in_specs=[pl.BlockSpec(memory_space=pltpu.HBM)] * 4,
        out_specs=(vmem,) * 4,
        scratch_shapes=[
            pltpu.VMEM((order, cols), f32),
            pltpu.VMEM((order, height), f32),
            pltpu.VMEM((n_mr, order, block_cols), f32),
            pltpu.VMEM((order, order), f32),
            pltpu.VMEM((order, height), f32),
            pltpu.VMEM((height + rows, order), jnp.bfloat16),
            pltpu.VMEM((height + rows, order), jnp.bfloat16),
            dma((3,)), dma((chunks,)),
            dma((3, levels + 1, chunks)), dma((2 * n_mc, chunks)),
            dma((n_mc,)), dma((n_mc,)), dma((n_mr,)), dma((n_mr,)), dma((n_mr,)), dma((n_mr,)),
        ],
        compiler_params=pltpu.CompilerParams(
            collective_id=0, has_side_effects=True, vmem_limit_bytes=VMEM_BYTES - held),
    )(column_panel.T, diag_block, row_panel, trailing)
    solved, inverse, scaled, updated = pl.pallas_call(
        store,
        out_shape=tuple(jax.ShapeDtypeStruct(part.shape, f32) for part in parts),
        in_specs=[vmem] * 4,
        out_specs=(anywhere,) * 4,
        scratch_shapes=[dma((3 + 8,))],
        compiler_params=pltpu.CompilerParams(vmem_limit_bytes=1024 * 1024),
    )(*parts)
    return solved.T, inverse, scaled, updated


def solution(mesh):
    placed = (P("mc", "mr"),) * 4
    return jax.shard_map(
        functools.partial(shards, mesh.shape["mc"], mesh.shape["mr"]),
        mesh=mesh, in_specs=placed, out_specs=placed, check_vma=False)
```

profile of v0, /device:TPU:0, one launch (start us, length us, event | category | flops | bytes accessed | tf_op | source)
XLA Modules:
  0.0 98.4 jit_solution(8846483247581796132)
XLA Ops:
  0.6 91.5 %shard_map.75 = (f32[64,512]{1,0:T(8,128)S(1)}, f32[32,64]{1,0:T(8,128)S(1)}, f32[32,8192]{1,0:T(8,128)S(1)}, f32[512,8192]{1,0:T(8,128)S(1)}) custom-call(f32[64,512]{1,0:T(8,128)} %bitcast.2, f32[32,64]{1,0:T(8,128)} %diag_ref.1, f32[32,8192]{1,0:T(8,128)} %row_ref.1, f32[512,8192]{1,0:T(8,128)} %trailing_ref.1), custom_call_target="tpu_custom_call" | custom-call | tf_op jit(solution)/shard_map/pallas_call | solution.py:343
  92.2 6.3 %shard_map.76 = (f32[64,512]{1,0:T(8,128)}, f32[32,64]{1,0:T(8,128)}, f32[32,8192]{1,0:T(8,128)}, f32[512,8192]{1,0:T(8,128)}) custom-call(f32[64,512]{1,0:T(8,128)S(1)} %get-tuple-element.12.refs_0_, f32[32,64]{1,0:T(8,128)S(1)} %get-tuple-element.13.refs_1_, f32[32,8192]{1,0:T(8,128)S(1)} %get-tuple-element.14.refs_2_, ...), custom_call_target="tpu_custom_call" | custom-call | tf_op jit(solution)/shard_map/pallas_call | solution.py:368
where the time goes:
time: 98.6 us; the launch traced here: 98.4 us
  Pallas kernels  97.8 us (99%)
    pallas_call x1, Pallas kernels, shards(): pl.pallas_call(functools.partial(kernel, n_mc, n_mr, chunks, tile), out_s...  91.5 us
    pallas_call x1, Pallas kernels, shards(): pl.pallas_call(store, out_shape=tuple((jax.ShapeDtypeStruct(part.shape, f...  6.28 us

commit v1 on v0

--- a/solution.py
+++ b/solution.py
@@ -43,7 +43,7 @@
            column_ref, diag_ref, row_ref, trailing_ref,
            solved_ref, inverse_ref, scaled_ref, updated_ref,
            panel, columns, diags, matrix, flipped, left_high, left_low,
-           load_sem, trail_sem, send_sem, recv_sem,
+           load_sem, row_sem, trail_sem, send_sem, recv_sem,
            diag_send, diag_recv, block_send, block_recv, col_send, col_recv):
     mc = lax.axis_index("mc")
     mr = lax.axis_index("mr")
@@ -60,24 +60,46 @@
     def at(mc_index, mr_index):
         return {"mc": mc_index, "mr": mr_index}
 
-    own_row = pltpu.make_async_copy(
-        row_ref, panel.at[pl.ds(pl.multiple_of(mc * rows, rows), rows)], load_sem.at[0])
+    down = jnp.maximum(mc - 2, 0)
+    up = jnp.minimum(mc + 2, n_mc - 1)
+    across = z * 2 + 1 - x
+    other = 1 - x
+    top = 2 * (levels - 1) + other
+    bottom = other
+
+    barrier = pltpu.get_barrier_semaphore()
+
+    def greet(mc_index, mr_index):
+        pl.semaphore_signal(barrier, inc=1, device_id=at(mc_index, mr_index),
+                            device_id_type=pl.DeviceIdType.MESH)
+
+    @pl.when(z > 0)
+    def _():
+        greet(down, mr)
+
+    @pl.when(z < levels - 1)
+    def _():
+        greet(up, mr)
+
+    greet(across, mr)
+    for step in range(1, n_mr):
+        greet(mc, lax.rem(mr + step, n_mr))
+
     own_diag = pltpu.make_async_copy(
-        diag_ref, diags.at[mr, pl.ds(pl.multiple_of(mc * rows, rows), rows)], load_sem.at[1])
+        diag_ref, diags.at[mr, pl.ds(pl.multiple_of(mc * rows, rows), rows)], load_sem.at[0])
     own_part = lambda k: pl.ds(pl.multiple_of(k * block_cols, block_cols), block_cols)
-    own_column = pltpu.make_async_copy(column_ref, columns.at[own_part(mr)], load_sem.at[2])
-    own_row.start()
+    own_column = pltpu.make_async_copy(column_ref, columns.at[own_part(mr)], load_sem.at[1])
+
+    def own_row(c):
+        part = pl.ds(pl.multiple_of(c * width, width), width)
+        return pltpu.make_async_copy(
+            row_ref.at[:, part], panel.at[pl.ds(pl.multiple_of(mc * rows, rows), rows), part], row_sem.at[c])
+
     own_diag.start()
+    for c in range(chunks):
+        own_row(c).start()
     own_column.start()
-
-    barrier = pltpu.get_barrier_semaphore()
-    for step in range(1, n_mc):
-        pl.semaphore_signal(barrier, inc=1, device_id=at(lax.rem(mc + step, n_mc), mr),
-                            device_id_type=pl.DeviceIdType.MESH)
-    for step in range(1, n_mr):
-        pl.semaphore_signal(barrier, inc=1, device_id=at(mc, lax.rem(mr + step, n_mr)),
-                            device_id_type=pl.DeviceIdType.MESH)
-    pl.semaphore_wait(barrier, n_mc + n_mr - 2)
+    pl.semaphore_wait(barrier, n_mr + jnp.where(z > 0, 1, 0) + jnp.where(z < levels - 1, 1, 0))
 
     def piece(shard, c, low=None):
         first = pl.multiple_of(shard * rows, rows)
@@ -95,14 +117,10 @@
             recv_sem=recv_sem.at[2 * shard + (1 if low == 1 else 0), c],
             device_id=at(target, mr), device_id_type=pl.DeviceIdType.MESH)
 
-    down = jnp.maximum(mc - 2, 0)
-    up = jnp.minimum(mc + 2, n_mc - 1)
-    across = z * 2 + 1 - x
-
-    def diag_copy(step, source, target):
-        ref = diags.at[mr, pl.ds(pl.multiple_of(source * rows, rows), rows)]
+    def diag_copy(shard, way, slot, target):
+        ref = diags.at[mr, pl.ds(pl.multiple_of(shard * rows, rows), rows)]
         return pltpu.make_async_remote_copy(
-            src_ref=ref, dst_ref=ref, send_sem=diag_send.at[step], recv_sem=diag_recv.at[step],
+            src_ref=ref, dst_ref=ref, send_sem=diag_send.at[way, slot], recv_sem=diag_recv.at[shard],
             device_id=at(target, mr), device_id_type=pl.DeviceIdType.MESH)
 
     def block_copy(step, source, target):
@@ -117,10 +135,9 @@
             src_ref=ref, dst_ref=ref, send_sem=col_send.at[step], recv_sem=col_recv.at[step],
             device_id=at(mc, target), device_id_type=pl.DeviceIdType.MESH)
 
-    own_row.wait()
-
-    @pl.loop(0, chunks)
-    def _(c):
+    def send_row(c):
+        own_row(c).wait()
+
         @pl.when(z > 0)
         def _():
             copy(mc, c, 0, z, down).start()
@@ -132,9 +149,17 @@
         copy(mc, c, 2, z, across).start()
 
     own_diag.wait()
-    for step in range(1, n_mc):
-        diag_copy(step, mc, lax.rem(mc + step, n_mc)).start()
-
+
+    @pl.when(z > 0)
+    def _():
+        diag_copy(mc, 0, z, down).start()
+
+    @pl.when(z < levels - 1)
+    def _():
+        diag_copy(mc, 1, z, up).start()
+
+    diag_copy(mc, 2, z, across).start()
+    send_row(0)
     own_column.wait()
     for step in range(1, n_mr):
         column_copy(step, mr, lax.rem(mr + step, n_mr)).start()
@@ -160,13 +185,39 @@
             act(copy(2 * q + x, c, 2, q, across))
 
     start = lambda d: d.start()
-    other = 1 - x
-    top = 2 * (levels - 1) + other
-    bottom = other
+
+    for hop in range(levels - 1):
+        above = z + 1 + hop
+        below = z - 1 - hop
+
+        @pl.when(above < levels)
+        def _():
+            diag_copy(2 * above + x, 0, above, down).wait_recv()
+
+            @pl.when(z > 0)
+            def _():
+                diag_copy(2 * above + x, 0, above, down).start()
+
+            diag_copy(2 * above + x, 2, above, across).start()
+
+        @pl.when(below >= 0)
+        def _():
+            diag_copy(2 * below + x, 1, below, up).wait_recv()
+
+            @pl.when(z < levels - 1)
+            def _():
+                diag_copy(2 * below + x, 1, below, up).start()
+
+            diag_copy(2 * below + x, 2, below, across).start()
+
+        if hop + 1 < chunks:
+            send_row(hop + 1)
+    for c in range(levels, chunks):
+        send_row(c)
 
     def invert():
-        for step in range(1, n_mc):
-            diag_copy(step, lax.rem(mc + n_mc - step, n_mc), lax.rem(mc + step, n_mc)).wait_recv()
+        for q in range(levels):
+            diag_copy(2 * q + other, 2, q, across).wait_recv()
         for step in range(1, n_mr):
             block_copy(step, mr, lax.rem(mr + step, n_mr)).start()
         for step in range(1, n_mr):
@@ -281,8 +332,16 @@
             updated_ref[:, part] = updated_ref[:, part] + product[0:height]
             scaled_ref[:, part] = product[height:height + rows]
 
-    for step in range(1, n_mc):
-        diag_copy(step, mc, lax.rem(mc + step, n_mc)).wait_send()
+    for q in range(levels):
+        @pl.when(jnp.logical_and(z > 0, z <= q))
+        def _():
+            diag_copy(2 * q + x, 0, q, down).wait_send()
+
+        @pl.when(jnp.logical_and(z < levels - 1, z >= q))
+        def _():
+            diag_copy(2 * q + x, 1, q, up).wait_send()
+
+        diag_copy(2 * q + x, 2, q, across).wait_send()
     for step in range(1, n_mr):
         block_copy(step, mr, lax.rem(mr + step, n_mr)).wait_send()
         column_copy(step, mr, lax.rem(mr + step, n_mr)).wait_send()
@@ -358,9 +417,9 @@
             pltpu.VMEM((order, height), f32),
             pltpu.VMEM((height + rows, order), jnp.bfloat16),
             pltpu.VMEM((height + rows, order), jnp.bfloat16),
-            dma((3,)), dma((chunks,)),
+            dma((2,)), dma((chunks,)), dma((chunks,)),
             dma((3, levels + 1, chunks)), dma((2 * n_mc, chunks)),
-            dma((n_mc,)), dma((n_mc,)), dma((n_mr,)), dma((n_mr,)), dma((n_mr,)), dma((n_mr,)),
+            dma((3, levels)), dma((n_mc,)), dma((n_mr,)), dma((n_mr,)), dma((n_mr,)), dma((n_mr,)),
         ],
         compiler_params=pltpu.CompilerParams(
             collective_id=0, has_side_effects=True, vmem_limit_bytes=VMEM_BYTES - held),

time: 98.6 us -> 96.2 us (0.976)
  Pallas kernels: 97.8 us -> 95.4 us
    pallas_call x1, Pallas kernels: 91.5 us -> 89.1 us  [shards(): pl.pallas_call(functools.partial(kernel, n_mc, n_mr, chunks, tile), out_s...]
where the time goes in v1:
time: 96.2 us; the launch traced here: 96.1 us
  Pallas kernels  95.4 us (99%)
    pallas_call x1, Pallas kernels, shards(): pl.pallas_call(functools.partial(kernel, n_mc, n_mr, chunks, tile), out_s...  89.1 us
    pallas_call x1, Pallas kernels, shards(): pl.pallas_call(store, out_shape=tuple((jax.ShapeDtypeStruct(part.shape, f...  6.28 us

profile of v1, /device:TPU:0, one launch (start us, length us, event | category | flops | bytes accessed | tf_op | source)
XLA Modules:
  0.0 96.1 jit_solution(4029217812299634661)
XLA Ops:
  0.6 89.1 %shard_map.75 = (f32[64,512]{1,0:T(8,128)S(1)}, f32[32,64]{1,0:T(8,128)S(1)}, f32[32,8192]{1,0:T(8,128)S(1)}, f32[512,8192]{1,0:T(8,128)S(1)}) custom-call(f32[64,512]{1,0:T(8,128)} %bitcast.2, f32[32,64]{1,0:T(8,128)} %diag_ref.1, f32[32,8192]{1,0:T(8,128)} %row_ref.1, f32[512,8192]{1,0:T(8,128)} %trailing_ref.1), custom_call_target="tpu_custom_call" | custom-call | tf_op jit(solution)/shard_map/pallas_call | solution.py:402
  89.8 6.3 %shard_map.76 = (f32[64,512]{1,0:T(8,128)}, f32[32,64]{1,0:T(8,128)}, f32[32,8192]{1,0:T(8,128)}, f32[512,8192]{1,0:T(8,128)}) custom-call(f32[64,512]{1,0:T(8,128)S(1)} %get-tuple-element.12.refs_0_, f32[32,64]{1,0:T(8,128)S(1)} %get-tuple-element.13.refs_1_, f32[32,8192]{1,0:T(8,128)S(1)} %get-tuple-element.14.refs_2_, ...), custom_call_target="tpu_custom_call" | custom-call | tf_op jit(solution)/shard_map/pallas_call | solution.py:427

commit v2 on v1

v2 whole, which is shorter than its diff:
```python
import functools

import jax
import jax.numpy as jnp
from jax import lax
from jax.experimental import pallas as pl
from jax.experimental.pallas import tpu as pltpu
from jax.sharding import PartitionSpec as P

VMEM_BYTES = 67043328
HIGHEST = lax.Precision.HIGHEST


def dot(a, b):
    return jnp.dot(a, b, precision=HIGHEST, preferred_element_type=jnp.float32)


def upper_inverse(matrix):
    order = matrix.shape[0]
    row = lax.broadcasted_iota(jnp.int32, (order, order), 0)
    col = lax.broadcasted_iota(jnp.int32, (order, order), 1)
    on_diag = row == col
    pivots = jnp.where(on_diag, matrix, 0.0)
    recip_col = 1.0 / jnp.sum(pivots, axis=1, keepdims=True)
    recip_row = 1.0 / jnp.sum(pivots, axis=0, keepdims=True)
    power = -(recip_col * jnp.where(col > row, matrix, 0.0))
    identity = jnp.where(on_diag, 1.0, 0.0)
    product = identity + power
    steps = max((order - 1).bit_length(), 1)
    for level in range(steps - 1):
        power = dot(power, power)
        product = dot(product, identity + power)
    return product * recip_row


def split(value):
    high = value.astype(jnp.bfloat16)
    low = (value - high.astype(jnp.float32)).astype(jnp.bfloat16)
    return high, low


def kernel(n_mc, n_mr, chunks, late, tile,
           column_ref, diag_ref, row_ref, trailing_ref,
           solved_ref, inverse_ref, scaled_ref, updated_ref, panel, left_high, left_low,
           columns, diags, matrix, flipped,
           load_sem, trail_sem, send_sem, line_recv, half_recv, pair_recv, rest_recv,
           diag_send, diag_recv, block_send, block_recv, col_send, col_recv):
    mc = lax.axis_index("mc")
    mr = lax.axis_index("mr")
    levels = n_mc // 2
    z = mc // 2
    x = lax.rem(mc, 2)
    rows = row_ref.shape[0]
    half = rows // 2
    cols = row_ref.shape[1]
    width = cols // chunks
    block_cols = diag_ref.shape[1]
    height = column_ref.shape[1]
    last = levels - 1

    def at(mc_index, mr_index):
        return {"mc": mc_index, "mr": mr_index}

    down = jnp.maximum(mc - 2, 0)
    up = jnp.minimum(mc + 2, n_mc - 1)
    across = z * 2 + 1 - x
    other = 1 - x
    top = 2 * last + other
    bottom = other

    barrier = pltpu.get_barrier_semaphore()

    def greet(mc_index, mr_index):
        pl.semaphore_signal(barrier, inc=1, device_id=at(mc_index, mr_index),
                            device_id_type=pl.DeviceIdType.MESH)

    @pl.when(z > 0)
    def _():
        greet(down, mr)

    @pl.when(z < last)
    def _():
        greet(up, mr)

    greet(across, mr)
    for step in range(1, n_mr):
        greet(mc, lax.rem(mr + step, n_mr))

    own_rows = pl.ds(pl.multiple_of(mc * rows, rows), rows)
    own_part = lambda k: pl.ds(pl.multiple_of(k * block_cols, block_cols), block_cols)
    own_diag = pltpu.make_async_copy(diag_ref, diags.at[mr, own_rows], load_sem.at[0])
    own_column = pltpu.make_async_copy(column_ref, columns.at[own_part(mr)], load_sem.at[1])
    own_first = pltpu.make_async_copy(
        row_ref.at[:, pl.ds(0, width)], panel.at[own_rows, pl.ds(0, width)], load_sem.at[2])
    own_diag.start()
    own_first.start()
    if chunks > 1:
        own_rest = pltpu.make_async_copy(
            row_ref.at[:, pl.ds(width, cols - width)], panel.at[own_rows, pl.ds(width, cols - width)],
            load_sem.at[3])
        own_rest.start()
    own_column.start()
    pl.semaphore_wait(barrier, n_mr + jnp.where(z > 0, 1, 0) + jnp.where(z < last, 1, 0))

    def remote(ref, send, recv, mc_index, mr_index):
        return pltpu.make_async_remote_copy(
            src_ref=ref, dst_ref=ref, send_sem=send, recv_sem=recv,
            device_id=at(mc_index, mr_index), device_id_type=pl.DeviceIdType.MESH)

    def piece(shard, c, low=None):
        first = pl.multiple_of(shard * rows, rows)
        count = rows
        if low is not None:
            first = pl.multiple_of(shard * rows + low * half, half)
            count = half
        return panel.at[pl.ds(first, count), pl.ds(pl.multiple_of(c * width, width), width)]

    target = (down, up, across)

    def line(q, c, way):
        return remote(piece(2 * q + x, c), send_sem.at[way], line_recv.at[q, c], target[way], mr)

    def split_piece(c, way):
        return remote(piece((top, bottom)[way], c, 1), send_sem.at[way], half_recv.at[way, c], target[way], mr)

    def pair(shard, c):
        return remote(piece(shard, c), send_sem.at[2], pair_recv.at[c], across, mr)

    def cross(q, c, low=None):
        return remote(piece(2 * q + x, c, low), send_sem.at[2], rest_recv.at[c], across, mr)

    def diag_line(q, way):
        ref = diags.at[mr, pl.ds(pl.multiple_of((2 * q + x) * rows, rows), rows)]
        return remote(ref, diag_send.at[way], diag_recv.at[q if way < 2 else levels], target[way], mr)

    def block_copy(k, step):
        return remote(diags.at[k], block_send.at[0], block_recv.at[0], mc, lax.rem(mr + step, n_mr))

    def column_copy(k, step):
        return remote(columns.at[own_part(k)], col_send.at[0], col_recv.at[0], mc, lax.rem(mr + step, n_mr))

    def send_row(c):
        @pl.when(z > 0)
        def _():
            line(z, c, 0).start()

        @pl.when(z < last)
        def _():
            line(z, c, 1).start()

        pair(mc, c).start()

    own_diag.wait()

    @pl.when(z > 0)
    def _():
        diag_line(z, 0).start()

    @pl.when(z < last)
    def _():
        diag_line(z, 1).start()

    diag_line(z, 2).start()
    own_first.wait()
    send_row(0)
    own_column.wait()
    for step in range(1, n_mr):
        column_copy(mr, step).start()
    if chunks > 1:
        own_rest.wait()
    load_trailing = pltpu.make_async_copy(trailing_ref, updated_ref, trail_sem.at[0])
    load_trailing.start()

    for hop in range(last):
        above = z + 1 + hop
        below = z - 1 - hop

        @pl.when(above < levels)
        def _():
            diag_line(above, 0).wait_recv()

            @pl.when(z > 0)
            def _():
                diag_line(above, 0).start()

            diag_line(above, 2).start()

        @pl.when(below >= 0)
        def _():
            diag_line(below, 1).wait_recv()

            @pl.when(z < last)
            def _():
                diag_line(below, 1).start()

            diag_line(below, 2).start()

        if hop + 1 < chunks:
            send_row(hop + 1)
    for c in range(levels, chunks):
        send_row(c)

    first_half_only = lambda q: jnp.logical_or(
        jnp.logical_and(q == last, z != last), jnp.logical_and(q == 0, z != 0))

    def send_across(q, c):
        @pl.when(first_half_only(q))
        def _():
            cross(q, c, 0).start()

        @pl.when(jnp.logical_not(first_half_only(q)))
        def _():
            cross(q, c).start()

    def invert():
        remote(diags.at[mr, pl.ds(0, levels * rows)], diag_send.at[2], diag_recv.at[levels], across, mr).wait_recv()
        for step in range(1, n_mr):
            block_copy(mr, step).start()
        remote(diags.at[pl.ds(0, n_mr - 1)], block_send.at[0], block_recv.at[0], mc, lax.rem(mr + 1, n_mr)).wait_recv()
        for k in range(n_mr):
            matrix[:, k * block_cols:(k + 1) * block_cols] = diags[k]
        matrix[...] = upper_inverse(matrix[...])
        own_inverse = matrix[own_rows, :]
        remote(columns.at[pl.ds(0, (n_mr - 1) * block_cols)], col_send.at[0], col_recv.at[0], mc,
               lax.rem(mr + 1, n_mr)).wait_recv()
        flipped[...] = -lax.dot_general(
            matrix[...], columns[...], (((0,), (0,)), ((), ())),
            precision=HIGHEST, preferred_element_type=jnp.float32)
        solved_ref[...] = flipped[own_part(mr), :]
        left_high[0:height, :], left_low[0:height, :] = split(flipped[...].T)
        left_high[height:height + rows, :], left_low[height:height + rows, :] = split(own_inverse)
        for k in range(n_mr):
            @pl.when(mr == k)
            def _():
                inverse_ref[...] = own_inverse[:, k * block_cols:(k + 1) * block_cols]

    for phase in range(last):
        if phase == min(1, levels - 2):
            invert()

        above = z + 1 + phase
        below = z - 1 - phase

        @pl.loop(0, chunks)
        def _(c):
            @pl.when(above < levels)
            def _():
                line(above, c, 0).wait_recv()

                @pl.when(z > 0)
                def _():
                    line(above, c, 0).start()

                send_across(above, c)

            @pl.when(below >= 0)
            def _():
                line(below, c, 1).wait_recv()

                @pl.when(z < last)
                def _():
                    line(below, c, 1).start()

                send_across(below, c)

            if phase == 0:
                pair(2 * z + other, c).wait_recv()

                @pl.when(z == last)
                def _():
                    split_piece(c, 0).start()

                @pl.when(z == 0)
                def _():
                    split_piece(c, 1).start()

            @pl.when(above == levels)
            def _():
                @pl.when(z < last)
                def _():
                    split_piece(c, 0).wait_recv()

                    @pl.when(z > 0)
                    def _():
                        split_piece(c, 0).start()

            @pl.when(below == -1)
            def _():
                @pl.when(z > 0)
                def _():
                    split_piece(c, 1).wait_recv()

                    @pl.when(z < last)
                    def _():
                        split_piece(c, 1).start()

    def receive_rest(c):
        @pl.when(z == 0)
        def _():
            split_piece(c, 0).wait_recv()

        @pl.when(z == last)
        def _():
            split_piece(c, 1).wait_recv()

        def gathered(halves):
            ref = panel.at[pl.ds(0, halves * half), pl.ds(0, width)]
            remote(ref, send_sem.at[2], rest_recv.at[c], across, mr).wait_recv()

        at_end = jnp.logical_or(z == 0, z == last)

        @pl.when(at_end)
        def _():
            gathered(2 * levels - 3)

        if levels > 2:
            @pl.when(jnp.logical_not(at_end))
            def _():
                gathered(2 * levels - 4)

    load_trailing.wait()

    @pl.loop(0, chunks - late)
    def _(c):
        receive_rest(c)
        for t in range(width // tile):
            part = pl.ds(pl.multiple_of(c * width + t * tile, tile), tile)
            product = multiply(left_high, left_low, panel[:, part])
            updated_ref[:, part] = updated_ref[:, part] + product[0:height]
            scaled_ref[:, part] = product[height:height + rows]

    for c in range(chunks - late, chunks):
        receive_rest(c)

    def sent(way, halves, diag_pieces):
        remote(panel.at[pl.ds(0, halves * half)], send_sem.at[way], pair_recv.at[0], target[way], mr).wait_send()
        remote(diags.at[mr, pl.ds(0, diag_pieces * rows)], diag_send.at[way], diag_recv.at[0], target[way],
               mr).wait_send()

    for k in range(levels):
        @pl.when(z == k)
        def _():
            if k > 0:
                sent(0, 2 * (levels - k) + 1, levels - k)
            if k < last:
                sent(1, 2 * (k + 1) + 1, k + 1)
            sent(2, 2 * levels - (1 if k in (0, last) else 2), levels)

    remote(diags.at[pl.ds(0, n_mr - 1)], block_send.at[0], block_recv.at[0], mc, lax.rem(mr + 1, n_mr)).wait_send()
    remote(columns.at[pl.ds(0, (n_mr - 1) * block_cols)], col_send.at[0], col_recv.at[0], mc,
           lax.rem(mr + 1, n_mr)).wait_send()


def multiply(left_high, left_low, right):
    right_high, right_low = split(right)
    product = jnp.dot(left_high[...], right_low, preferred_element_type=jnp.float32)
    product += jnp.dot(left_low[...], right_high, preferred_element_type=jnp.float32)
    return product + jnp.dot(left_high[...], right_high, preferred_element_type=jnp.float32)


def finish(done, tile, solved, inverse, scaled, updated, panel, left_high, left_low,
           solved_out, inverse_out, scaled_out, updated_out, held_updated, held_scaled, sem, tile_sem):
    height, cols = updated.shape
    strips = sem.shape[0] - 3
    deep = height // strips
    ready = pl.ds(0, done)
    copies = []
    for i in range(strips):
        part = pl.ds(i * deep, deep)
        copies.append(pltpu.make_async_copy(updated.at[part, ready], updated_out.at[part, ready], sem.at[3 + i]))
    copies.append(pltpu.make_async_copy(solved, solved_out, sem.at[0]))
    copies.append(pltpu.make_async_copy(inverse, inverse_out, sem.at[1]))
    copies.append(pltpu.make_async_copy(scaled.at[:, ready], scaled_out.at[:, ready], sem.at[2]))
    for c in copies:
        c.start()
    for t in range((cols - done) // tile):
        part = pl.ds(done + t * tile, tile)
        slot = pl.ds(t * tile, tile)
        product = multiply(left_high, left_low, panel[:, part])
        held_updated[:, slot] = updated[:, part] + product[0:height]
        held_scaled[:, slot] = product[height:]
        copies.append(pltpu.make_async_copy(held_updated.at[:, slot], updated_out.at[:, part], tile_sem.at[0, t]))
        copies.append(pltpu.make_async_copy(held_scaled.at[:, slot], scaled_out.at[:, part], tile_sem.at[1, t]))
        copies[-2].start()
        copies[-1].start()
    for c in copies:
        c.wait()


def shards(n_mc, n_mr, column_panel, diag_block, row_panel, trailing):
    rows, block_cols = diag_block.shape
    height, cols = trailing.shape
    order = rows * n_mc
    levels = n_mc // 2
    chunks = max(1, 16 // levels)
    while cols % (chunks * 128):
        chunks //= 2
    late = 1 if chunks > 1 else 0
    width = cols // chunks
    done = cols - late * width
    tile = 512 if width % 512 == 0 else 128
    held = 4 * (height * cols + rows * cols + block_cols * height + rows * 128 + order * cols
                + (height + rows) * order) + 64 * 1024
    dma = pltpu.SemaphoreType.DMA
    f32 = jnp.float32
    anywhere = pl.BlockSpec(memory_space=pl.ANY)
    vmem = pl.BlockSpec(memory_space=pltpu.VMEM)
    parts = pl.pallas_call(
        functools.partial(kernel, n_mc, n_mr, chunks, late, tile),
        out_shape=(
            pltpu.VMEM((block_cols, height), f32),
            pltpu.VMEM(diag_block.shape, f32),
            pltpu.VMEM(row_panel.shape, f32),
            pltpu.VMEM(trailing.shape, f32),
            pltpu.VMEM((order, cols), f32),
            pltpu.VMEM((height + rows, order), jnp.bfloat16),
            pltpu.VMEM((height + rows, order), jnp.bfloat16),
        ),
        in_specs=[pl.BlockSpec(memory_space=pltpu.HBM)] * 4,
        out_specs=(vmem,) * 7,
        scratch_shapes=[
            pltpu.VMEM((order, height), f32),
            pltpu.VMEM((n_mr, order, block_cols), f32),
            pltpu.VMEM((order, order), f32),
            pltpu.VMEM((order, height), f32),
            dma((4,)), dma((1,)), dma((3,)), dma((levels, chunks)), dma((2, chunks)), dma((chunks,)), dma((chunks,)),
            dma((3,)), dma((levels + 1,)), dma((1,)), dma((1,)), dma((1,)), dma((1,)),
        ],
        compiler_params=pltpu.CompilerParams(
            collective_id=0, has_side_effects=True, vmem_limit_bytes=VMEM_BYTES - held),
    )(column_panel.T, diag_block, row_panel, trailing)
    tiles = max(1, (cols - done) // tile)
    spare = max(tile, cols - done)
    solved, inverse, scaled, updated = pl.pallas_call(
        functools.partial(finish, done, tile),
        out_shape=tuple(jax.ShapeDtypeStruct(part.shape, f32) for part in parts[:4]),
        in_specs=[vmem] * 7,
        out_specs=(anywhere,) * 4,
        scratch_shapes=[pltpu.VMEM((height, spare), f32), pltpu.VMEM((rows, spare), f32), dma((3 + 8,)),
                        dma((2, tiles))],
        compiler_params=pltpu.CompilerParams(vmem_limit_bytes=4 * (height + rows) * (spare + 4 * tile) + 1024 * 1024),
    )(*parts)
    return solved.T, inverse, scaled, updated


def solution(mesh):
    placed = (P("mc", "mr"),) * 4
    return jax.shard_map(
        functools.partial(shards, mesh.shape["mc"], mesh.shape["mr"]),
        mesh=mesh, in_specs=placed, out_specs=placed, check_vma=False)
```

time: 96.2 us -> 93.2 us (0.969)
  Pallas kernels: 95.4 us -> 92.4 us
    pallas_call x2, Pallas kernels: 95.4 us -> 92.4 us  [the longest x1 86.1 us: shards(): pl.pallas_call(functools.partial(kernel, n_mc, n_mr, chunks, late, tile),...]
where the time goes in v2:
time: 93.2 us; the launch traced here: 93.1 us
  Pallas kernels  92.4 us (99%)
    pallas_call x1, Pallas kernels, shards(): pl.pallas_call(functools.partial(kernel, n_mc, n_mr, chunks, late, tile),...  86.1 us
    pallas_call x1, Pallas kernels, shards(): pl.pallas_call(functools.partial(finish, done, tile), out_shape=tuple((ja...  6.38 us

profile of v2, /device:TPU:0, one launch (start us, length us, event | category | flops | bytes accessed | tf_op | source)
XLA Modules:
  0.0 93.1 jit_solution(17344094864774201463)
XLA Ops:
  0.6 86.1 %shard_map.75 = (f32[64,512]{1,0:T(8,128)S(1)}, f32[32,64]{1,0:T(8,128)S(1)}, f32[32,8192]{1,0:T(8,128)S(1)}, f32[512,8192]{1,0:T(8,128)S(1)}, f32[256,8192]{1,0...) custom-call(f32[64,512]{1,0:T(8,128)} %bitcast.2, f32[32,64]{1,0:T(8,128)} %diag_ref.1, ...), custom_call_target="tpu_custom_call" | custom-call | tf_op jit(solution)/shard_map/pallas_call | solution.py:408
  86.7 6.4 %shard_map.76 = (f32[64,512]{1,0:T(8,128)}, f32[32,64]{1,0:T(8,128)}, f32[32,8192]{1,0:T(8,128)}, f32[512,8192]{1,0:T(8,128)}) custom-call(f32[64,512]{1,0:T(8,128)S(1)} %get-tuple-element.15.solved, f32[32,64]{1,0:T(8,128)S(1)} %get-tuple-element.16.inverse, f32[32,8192]{1,0:T(8,128)S(1)} %get-tuple-element.17.scaled, ...), custom_call_target="tpu_custom_call" | custom-call | tf_op jit(solution)/shard_map/pallas_call | solution.py:434

commit v3 on v2

--- a/solution.py
+++ b/solution.py
@@ -39,12 +39,12 @@
     return high, low
 
 
-def kernel(n_mc, n_mr, chunks, late, tile,
+def kernel(n_mc, n_mr, chunks, late, tile, detour,
            column_ref, diag_ref, row_ref, trailing_ref,
            solved_ref, inverse_ref, scaled_ref, updated_ref, panel, left_high, left_low,
-           columns, diags, matrix, flipped,
+           columns, diags, matrix, flipped, carried,
            load_sem, trail_sem, send_sem, line_recv, half_recv, pair_recv, rest_recv,
-           diag_send, diag_recv, block_send, block_recv, col_send, col_recv):
+           diag_send, diag_recv, block_send, block_recv, col_send, col_recv, own_send, carry_send, carry_recv):
     mc = lax.axis_index("mc")
     mr = lax.axis_index("mr")
     levels = n_mc // 2
@@ -57,6 +57,11 @@
     block_cols = diag_ref.shape[1]
     height = column_ref.shape[1]
     last = levels - 1
+    final = chunks - 1
+    kept = width - detour
+    per = block_cols // (2 * rows) if block_cols % (2 * rows) == 0 else levels
+    needed = lambda m: jnp.minimum(levels, (m + 1) * per)
+    limit = needed(mr)
 
     def at(mc_index, mr_index):
         return {"mc": mc_index, "mr": mr_index}
@@ -107,24 +112,26 @@
             src_ref=ref, dst_ref=ref, send_sem=send, recv_sem=recv,
             device_id=at(mc_index, mr_index), device_id_type=pl.DeviceIdType.MESH)
 
-    def piece(shard, c, low=None):
+    def piece(shard, c, low=None, span=None):
         first = pl.multiple_of(shard * rows, rows)
         count = rows
         if low is not None:
             first = pl.multiple_of(shard * rows + low * half, half)
             count = half
-        return panel.at[pl.ds(first, count), pl.ds(pl.multiple_of(c * width, width), width)]
+        return panel.at[pl.ds(first, count), pl.ds(pl.multiple_of(c * width, width), span or width)]
 
     target = (down, up, across)
 
-    def line(q, c, way):
-        return remote(piece(2 * q + x, c), send_sem.at[way], line_recv.at[q, c], target[way], mr)
+    def line(q, c, way, send=None, span=None):
+        return remote(piece(2 * q + x, c, None, span), send_sem.at[way] if send is None else send,
+                      line_recv.at[q, c], target[way], mr)
 
     def split_piece(c, way):
         return remote(piece((top, bottom)[way], c, 1), send_sem.at[way], half_recv.at[way, c], target[way], mr)
 
-    def pair(shard, c):
-        return remote(piece(shard, c), send_sem.at[2], pair_recv.at[c], across, mr)
+    def pair(shard, c, send=None, span=None):
+        return remote(piece(shard, c, None, span), send_sem.at[2] if send is None else send,
+                      pair_recv.at[c], across, mr)
 
     def cross(q, c, low=None):
         return remote(piece(2 * q + x, c, low), send_sem.at[2], rest_recv.at[c], across, mr)
@@ -140,34 +147,82 @@
         return remote(columns.at[own_part(k)], col_send.at[0], col_recv.at[0], mc, lax.rem(mr + step, n_mr))
 
     def send_row(c):
-        @pl.when(z > 0)
-        def _():
-            line(z, c, 0).start()
-
-        @pl.when(z < last)
-        def _():
-            line(z, c, 1).start()
-
-        pair(mc, c).start()
+        def send(span):
+            send = own_send.at[0] if c == final else None
+
+            @pl.when(z > 0)
+            def _():
+                line(z, c, 0, send, span).start()
+
+            @pl.when(z < last)
+            def _():
+                line(z, c, 1, send, span).start()
+
+            pair(mc, c, send, span).start()
+
+        if c == final and detour:
+            by_mr(lambda: send(kept), lambda: send(width))
+        else:
+            send(width)
+
+    def by_mr(first, others):
+        pl.when(mr == 0)(first)
+        pl.when(mr != 0)(others)
+
+    sides = (z > 0, z < last, None)
+
+    def each_side(act):
+        for way in range(3):
+            if sides[way] is None:
+                act(way)
+            else:
+                pl.when(sides[way])(functools.partial(act, way))
+
+    def detoured(shard):
+        return panel.at[pl.ds(pl.multiple_of(shard * rows, rows), rows), pl.ds(final * width + kept, detour)]
+
+    def carry_out():
+        return pltpu.make_async_remote_copy(
+            src_ref=detoured(mc), dst_ref=carried.at[0], send_sem=carry_send.at[0], recv_sem=carry_recv.at[0],
+            device_id=at(mc, n_mr - 1), device_id_type=pl.DeviceIdType.MESH)
+
+    def carry_on(way):
+        return pltpu.make_async_remote_copy(
+            src_ref=carried.at[0], dst_ref=carried.at[1 + way], send_sem=carry_send.at[0],
+            recv_sem=carry_recv.at[1 + way], device_id=at(target[way], mr), device_id_type=pl.DeviceIdType.MESH)
+
+    def carry_home(way):
+        shard = (mc + 2, mc - 2, across)[way]
+        return pltpu.make_async_remote_copy(
+            src_ref=carried.at[1 + way], dst_ref=detoured(shard), send_sem=carry_send.at[1],
+            recv_sem=carry_recv.at[1 + way], device_id=at(mc, 0), device_id_type=pl.DeviceIdType.MESH)
+
+    sources = (z < last, z > 0, None)
+
+    def each_source(act):
+        for way in range(3):
+            if sources[way] is None:
+                act(way)
+            else:
+                pl.when(sources[way])(functools.partial(act, way))
 
     own_diag.wait()
 
-    @pl.when(z > 0)
+    @pl.when(z < limit)
     def _():
-        diag_line(z, 0).start()
-
-    @pl.when(z < last)
-    def _():
-        diag_line(z, 1).start()
-
-    diag_line(z, 2).start()
+        each_side(lambda way: diag_line(z, way).start())
+
     own_first.wait()
     send_row(0)
+    if chunks > 1:
+        own_rest.wait()
+    if detour:
+        @pl.when(mr == 0)
+        def _():
+            carry_out().start()
     own_column.wait()
     for step in range(1, n_mr):
         column_copy(mr, step).start()
-    if chunks > 1:
-        own_rest.wait()
     load_trailing = pltpu.make_async_copy(trailing_ref, updated_ref, trail_sem.at[0])
     load_trailing.start()
 
@@ -175,7 +230,7 @@
         above = z + 1 + hop
         below = z - 1 - hop
 
-        @pl.when(above < levels)
+        @pl.when(above < limit)
         def _():
             diag_line(above, 0).wait_recv()
 
@@ -185,7 +240,7 @@
 
             diag_line(above, 2).start()
 
-        @pl.when(below >= 0)
+        @pl.when(jnp.logical_and(below >= 0, below < limit))
         def _():
             diag_line(below, 1).wait_recv()
 
@@ -195,10 +250,23 @@
 
             diag_line(below, 2).start()
 
+        if hop == 0 and detour:
+            @pl.when(mr == n_mr - 1)
+            def _():
+                carry_out().wait_recv()
+                each_side(lambda way: carry_on(way).start())
         if hop + 1 < chunks:
             send_row(hop + 1)
     for c in range(levels, chunks):
         send_row(c)
+    if detour:
+        @pl.when(mr == n_mr - 1)
+        def _():
+            def pass_home(way):
+                carry_on(way).wait_recv()
+                carry_home(way).start()
+
+            each_source(pass_home)
 
     first_half_only = lambda q: jnp.logical_or(
         jnp.logical_and(q == last, z != last), jnp.logical_and(q == 0, z != 0))
@@ -213,7 +281,11 @@
             cross(q, c).start()
 
     def invert():
-        remote(diags.at[mr, pl.ds(0, levels * rows)], diag_send.at[2], diag_recv.at[levels], across, mr).wait_recv()
+        for m in range(n_mr):
+            @pl.when(mr == m)
+            def _():
+                ref = diags.at[m, pl.ds(0, min(levels, (m + 1) * per) * rows)]
+                remote(ref, diag_send.at[2], diag_recv.at[levels], across, mr).wait_recv()
         for step in range(1, n_mr):
             block_copy(mr, step).start()
         remote(diags.at[pl.ds(0, n_mr - 1)], block_send.at[0], block_recv.at[0], mc, lax.rem(mr + 1, n_mr)).wait_recv()
@@ -241,11 +313,10 @@
         above = z + 1 + phase
         below = z - 1 - phase
 
-        @pl.loop(0, chunks)
-        def _(c):
+        def step(c, arrive):
             @pl.when(above < levels)
             def _():
-                line(above, c, 0).wait_recv()
+                arrive(0, lambda span: line(above, c, 0, None, span))
 
                 @pl.when(z > 0)
                 def _():
@@ -255,7 +326,7 @@
 
             @pl.when(below >= 0)
             def _():
-                line(below, c, 1).wait_recv()
+                arrive(1, lambda span: line(below, c, 1, None, span))
 
                 @pl.when(z < last)
                 def _():
@@ -264,7 +335,7 @@
                 send_across(below, c)
 
             if phase == 0:
-                pair(2 * z + other, c).wait_recv()
+                arrive(2, lambda span: pair(2 * z + other, c, None, span))
 
                 @pl.when(z == last)
                 def _():
@@ -293,6 +364,21 @@
                     @pl.when(z < last)
                     def _():
                         split_piece(c, 1).start()
+
+        def whole(way, make):
+            make(width).wait_recv()
+
+        def joined(way, make):
+            def first():
+                make(kept).wait_recv()
+                carry_home(way).wait_recv()
+
+            by_mr(first, lambda: make(width).wait_recv())
+
+        split_last = phase == 0 and detour > 0
+        pl.loop(0, chunks - 1 if split_last else chunks)(lambda c: step(c, whole))
+        if split_last:
+            step(final, joined)
 
     def receive_rest(c):
         @pl.when(z == 0)
@@ -332,19 +418,54 @@
     for c in range(chunks - late, chunks):
         receive_rest(c)
 
-    def sent(way, halves, diag_pieces):
-        remote(panel.at[pl.ds(0, halves * half)], send_sem.at[way], pair_recv.at[0], target[way], mr).wait_send()
-        remote(diags.at[mr, pl.ds(0, diag_pieces * rows)], diag_send.at[way], diag_recv.at[0], target[way],
-               mr).wait_send()
+    def sent(way, halves):
+        ref = panel.at[pl.ds(0, halves * half - rows // chunks)]
+        remote(ref, send_sem.at[way], pair_recv.at[0], target[way], mr).wait_send()
+
+    def sent_own(count, span):
+        ref = panel.at[pl.ds(0, count * rows), pl.ds(0, span)]
+        remote(ref, own_send.at[0], pair_recv.at[0], across, mr).wait_send()
+
+    def sent_diag(way, count):
+        if count > 0:
+            ref = diags.at[mr, pl.ds(0, count * rows)]
+            remote(ref, diag_send.at[way], diag_recv.at[0], target[way], mr).wait_send()
+
+    def sent_carry(slot, count):
+        remote(carried.at[pl.ds(0, count)], carry_send.at[slot], carry_recv.at[0], across, mr).wait_send()
 
     for k in range(levels):
         @pl.when(z == k)
         def _():
+            count = 1 + (k > 0) + (k < last)
             if k > 0:
-                sent(0, 2 * (levels - k) + 1, levels - k)
+                sent(0, 2 * (levels - k) + 1)
             if k < last:
-                sent(1, 2 * (k + 1) + 1, k + 1)
-            sent(2, 2 * levels - (1 if k in (0, last) else 2), levels)
+                sent(1, 2 * (k + 1) + 1)
+            sent(2, 2 * levels - (1 if k in (0, last) else 2))
+            if detour:
+                by_mr(lambda: sent_own(count, kept), lambda: sent_own(count, width))
+
+                @pl.when(mr == n_mr - 1)
+                def _():
+                    sent_carry(0, count)
+                    sent_carry(1, count)
+            else:
+                sent_own(count, width)
+            for m in range(n_mr):
+                @pl.when(mr == m)
+                def _():
+                    most = min(levels, (m + 1) * per)
+                    if k > 0:
+                        sent_diag(0, most - k)
+                    if k < last:
+                        sent_diag(1, min(k + 1, most))
+                    sent_diag(2, most)
+
+    if detour:
+        @pl.when(mr == 0)
+        def _():
+            sent_carry(0, 1)
 
     remote(diags.at[pl.ds(0, n_mr - 1)], block_send.at[0], block_recv.at[0], mc, lax.rem(mr + 1, n_mr)).wait_send()
     remote(columns.at[pl.ds(0, (n_mr - 1) * block_cols)], col_send.at[0], col_recv.at[0], mc,
@@ -399,6 +520,7 @@
     width = cols // chunks
     done = cols - late * width
     tile = 512 if width % 512 == 0 else 128
+    detour = 3 * width // 2048 * 128 if n_mr > 1 and chunks > 1 and levels > 1 else 0
     held = 4 * (height * cols + rows * cols + block_cols * height + rows * 128 + order * cols
                 + (height + rows) * order) + 64 * 1024
     dma = pltpu.SemaphoreType.DMA
@@ -406,7 +528,7 @@
     anywhere = pl.BlockSpec(memory_space=pl.ANY)
     vmem = pl.BlockSpec(memory_space=pltpu.VMEM)
     parts = pl.pallas_call(
-        functools.partial(kernel, n_mc, n_mr, chunks, late, tile),
+        functools.partial(kernel, n_mc, n_mr, chunks, late, tile, detour),
         out_shape=(
             pltpu.VMEM((block_cols, height), f32),
             pltpu.VMEM(diag_block.shape, f32),
@@ -423,8 +545,10 @@
             pltpu.VMEM((n_mr, order, block_cols), f32),
             pltpu.VMEM((order, order), f32),
             pltpu.VMEM((order, height), f32),
+            pltpu.VMEM((4, rows, max(detour, 128)), f32),
             dma((4,)), dma((1,)), dma((3,)), dma((levels, chunks)), dma((2, chunks)), dma((chunks,)), dma((chunks,)),
             dma((3,)), dma((levels + 1,)), dma((1,)), dma((1,)), dma((1,)), dma((1,)),
+            dma((1,)), dma((2,)), dma((4,)),
         ],
         compiler_params=pltpu.CompilerParams(
             collective_id=0, has_side_effects=True, vmem_limit_bytes=VMEM_BYTES - held),

time: 93.2 us -> 91.8 us (0.985)
  Pallas kernels: 92.4 us -> 91 us
    pallas_call x1, Pallas kernels: 86.1 us -> 84.6 us  [shards(): pl.pallas_call(functools.partial(kernel, n_mc, n_mr, chunks, late, tile,...]
where the time goes in v3:
time: 91.8 us; the launch traced here: 91.6 us
  Pallas kernels  91 us (99%)
    pallas_call x1, Pallas kernels, shards(): pl.pallas_call(functools.partial(kernel, n_mc, n_mr, chunks, late, tile,...  84.6 us
    pallas_call x1, Pallas kernels, shards(): pl.pallas_call(functools.partial(finish, done, tile), out_shape=tuple((ja...  6.38 us

profile of v3, /device:TPU:0, one launch (start us, length us, event | category | flops | bytes accessed | tf_op | source)
XLA Modules:
  0.0 91.6 jit_solution(17953510400696078048)
XLA Ops:
  0.6 84.6 %shard_map.75 = (f32[64,512]{1,0:T(8,128)S(1)}, f32[32,64]{1,0:T(8,128)S(1)}, f32[32,8192]{1,0:T(8,128)S(1)}, f32[512,8192]{1,0:T(8,128)S(1)}, f32[256,8192]{1,0...) custom-call(f32[64,512]{1,0:T(8,128)} %bitcast.2, f32[32,64]{1,0:T(8,128)} %diag_ref.1, ...), custom_call_target="tpu_custom_call" | custom-call | tf_op jit(solution)/shard_map/pallas_call | solution.py:530
  85.3 6.4 %shard_map.76 = (f32[64,512]{1,0:T(8,128)}, f32[32,64]{1,0:T(8,128)}, f32[32,8192]{1,0:T(8,128)}, f32[512,8192]{1,0:T(8,128)}) custom-call(f32[64,512]{1,0:T(8,128)S(1)} %get-tuple-element.15.solved, f32[32,64]{1,0:T(8,128)S(1)} %get-tuple-element.16.inverse, f32[32,8192]{1,0:T(8,128)S(1)} %get-tuple-element.17.scaled, ...), custom_call_target="tpu_custom_call" | custom-call | tf_op jit(solution)/shard_map/pallas_call | solution.py:558

commit v4 on v3

--- a/solution.py
+++ b/solution.py
@@ -44,7 +44,8 @@
            solved_ref, inverse_ref, scaled_ref, updated_ref, panel, left_high, left_low,
            columns, diags, matrix, flipped, carried,
            load_sem, trail_sem, send_sem, line_recv, half_recv, pair_recv, rest_recv,
-           diag_send, diag_recv, block_send, block_recv, col_send, col_recv, own_send, carry_send, carry_recv):
+           diag_send, diag_recv, block_send, block_recv, col_send, col_recv, own_send, carry_send, carry_recv,
+           ready_sem):
     mc = lax.axis_index("mc")
     mr = lax.axis_index("mr")
     levels = n_mc // 2
@@ -88,8 +89,15 @@
         greet(up, mr)
 
     greet(across, mr)
-    for step in range(1, n_mr):
-        greet(mc, lax.rem(mr + step, n_mr))
+    twins = n_mr // 2 - 1 if n_mr % 2 == 0 else 0
+    if n_mr % 2 == 0:
+        greet(mc, mr + 1 - 2 * lax.rem(mr, 2))
+        for step in range(2, n_mr, 2):
+            greet(mc, lax.rem(mr + step, n_mr))
+    else:
+        for step in range(1, n_mr):
+            greet(mc, lax.rem(mr + step, n_mr))
+    greeted = 2 + twins if n_mr % 2 == 0 else n_mr
 
     own_rows = pl.ds(pl.multiple_of(mc * rows, rows), rows)
     own_part = lambda k: pl.ds(pl.multiple_of(k * block_cols, block_cols), block_cols)
@@ -105,7 +113,7 @@
             load_sem.at[3])
         own_rest.start()
     own_column.start()
-    pl.semaphore_wait(barrier, n_mr + jnp.where(z > 0, 1, 0) + jnp.where(z < last, 1, 0))
+    pl.semaphore_wait(barrier, greeted + jnp.where(z > 0, 1, 0) + jnp.where(z < last, 1, 0))
 
     def remote(ref, send, recv, mc_index, mr_index):
         return pltpu.make_async_remote_copy(
@@ -124,7 +132,7 @@
 
     def line(q, c, way, send=None, span=None):
         return remote(piece(2 * q + x, c, None, span), send_sem.at[way] if send is None else send,
-                      line_recv.at[q, c], target[way], mr)
+                      line_recv.at[q - 1 if way == 0 else q, c], target[way], mr)
 
     def split_piece(c, way):
         return remote(piece((top, bottom)[way], c, 1), send_sem.at[way], half_recv.at[way, c], target[way], mr)
@@ -214,8 +222,14 @@
 
     own_first.wait()
     send_row(0)
+    if twins:
+        for step in range(2, n_mr, 2):
+            pl.semaphore_signal(ready_sem.at[0], inc=1, device_id=at(mc, lax.rem(mr + step, n_mr)),
+                                device_id_type=pl.DeviceIdType.MESH)
     if chunks > 1:
         own_rest.wait()
+    if twins:
+        pl.semaphore_wait(ready_sem.at[0], twins)
     if detour:
         @pl.when(mr == 0)
         def _():
@@ -480,30 +494,34 @@
 
 
 def finish(done, tile, solved, inverse, scaled, updated, panel, left_high, left_low,
-           solved_out, inverse_out, scaled_out, updated_out, held_updated, held_scaled, sem, tile_sem):
+           solved_out, inverse_out, scaled_out, updated_out, held_updated, held_scaled, sem):
     height, cols = updated.shape
-    strips = sem.shape[0] - 3
+    strips = 8
     deep = height // strips
     ready = pl.ds(0, done)
-    copies = []
+    rest = pl.ds(done, cols - done)
     for i in range(strips):
         part = pl.ds(i * deep, deep)
-        copies.append(pltpu.make_async_copy(updated.at[part, ready], updated_out.at[part, ready], sem.at[3 + i]))
-    copies.append(pltpu.make_async_copy(solved, solved_out, sem.at[0]))
-    copies.append(pltpu.make_async_copy(inverse, inverse_out, sem.at[1]))
-    copies.append(pltpu.make_async_copy(scaled.at[:, ready], scaled_out.at[:, ready], sem.at[2]))
+        pltpu.make_async_copy(updated.at[part, ready], updated_out.at[part, ready], sem.at[3]).start()
+    copies = [
+        pltpu.make_async_copy(solved, solved_out, sem.at[0]),
+        pltpu.make_async_copy(inverse, inverse_out, sem.at[1]),
+        pltpu.make_async_copy(scaled.at[:, ready], scaled_out.at[:, ready], sem.at[2]),
+    ]
     for c in copies:
         c.start()
+    copies.append(pltpu.make_async_copy(updated.at[:, ready], updated_out.at[:, ready], sem.at[3]))
     for t in range((cols - done) // tile):
         part = pl.ds(done + t * tile, tile)
         slot = pl.ds(t * tile, tile)
         product = multiply(left_high, left_low, panel[:, part])
         held_updated[:, slot] = updated[:, part] + product[0:height]
         held_scaled[:, slot] = product[height:]
-        copies.append(pltpu.make_async_copy(held_updated.at[:, slot], updated_out.at[:, part], tile_sem.at[0, t]))
-        copies.append(pltpu.make_async_copy(held_scaled.at[:, slot], scaled_out.at[:, part], tile_sem.at[1, t]))
-        copies[-2].start()
-        copies[-1].start()
+        pltpu.make_async_copy(held_updated.at[:, slot], updated_out.at[:, part], sem.at[4]).start()
+        pltpu.make_async_copy(held_scaled.at[:, slot], scaled_out.at[:, part], sem.at[5]).start()
+    if done < cols:
+        copies.append(pltpu.make_async_copy(held_updated, updated_out.at[:, rest], sem.at[4]))
+        copies.append(pltpu.make_async_copy(held_scaled, scaled_out.at[:, rest], sem.at[5]))
     for c in copies:
         c.wait()
 
@@ -520,7 +538,7 @@
     width = cols // chunks
     done = cols - late * width
     tile = 512 if width % 512 == 0 else 128
-    detour = 3 * width // 2048 * 128 if n_mr > 1 and chunks > 1 and levels > 1 else 0
+    detour = width // 1024 * 128 if n_mr > 1 and chunks > 1 and levels > 1 else 0
     held = 4 * (height * cols + rows * cols + block_cols * height + rows * 128 + order * cols
                 + (height + rows) * order) + 64 * 1024
     dma = pltpu.SemaphoreType.DMA
@@ -546,22 +564,20 @@
             pltpu.VMEM((order, order), f32),
             pltpu.VMEM((order, height), f32),
             pltpu.VMEM((4, rows, max(detour, 128)), f32),
-            dma((4,)), dma((1,)), dma((3,)), dma((levels, chunks)), dma((2, chunks)), dma((chunks,)), dma((chunks,)),
+            dma((4,)), dma((1,)), dma((3,)), dma((max(1, levels - 1), chunks)), dma((2, chunks)), dma((chunks,)), dma((chunks,)),
             dma((3,)), dma((levels + 1,)), dma((1,)), dma((1,)), dma((1,)), dma((1,)),
-            dma((1,)), dma((2,)), dma((4,)),
+            dma((1,)), dma((2,)), dma((4,)), pltpu.SemaphoreType.REGULAR((1,)),
         ],
         compiler_params=pltpu.CompilerParams(
             collective_id=0, has_side_effects=True, vmem_limit_bytes=VMEM_BYTES - held),
     )(column_panel.T, diag_block, row_panel, trailing)
-    tiles = max(1, (cols - done) // tile)
     spare = max(tile, cols - done)
     solved, inverse, scaled, updated = pl.pallas_call(
         functools.partial(finish, done, tile),
         out_shape=tuple(jax.ShapeDtypeStruct(part.shape, f32) for part in parts[:4]),
         in_specs=[vmem] * 7,
         out_specs=(anywhere,) * 4,
-        scratch_shapes=[pltpu.VMEM((height, spare), f32), pltpu.VMEM((rows, spare), f32), dma((3 + 8,)),
-                        dma((2, tiles))],
+        scratch_shapes=[pltpu.VMEM((height, spare), f32), pltpu.VMEM((rows, spare), f32), dma((6,))],
         compiler_params=pltpu.CompilerParams(vmem_limit_bytes=4 * (height + rows) * (spare + 4 * tile) + 1024 * 1024),
     )(*parts)
     return solved.T, inverse, scaled, updated

time: 91.8 us -> 91.4 us (level)
  no operation moved by 1% of the time
where the time goes in v4:
time: 91.4 us; the launch traced here: 91.2 us
  Pallas kernels  90.6 us (99%)
    pallas_call x1, Pallas kernels, shards(): pl.pallas_call(functools.partial(kernel, n_mc, n_mr, chunks, late, tile,...  84.3 us
    pallas_call x1, Pallas kernels, shards(): pl.pallas_call(functools.partial(finish, done, tile), out_shape=tuple((ja...  6.26 us

profile of v4, /device:TPU:0, one launch (start us, length us, event | category | flops | bytes accessed | tf_op | source)
XLA Modules:
  0.0 91.2 jit_solution(12200987917219328185)
XLA Ops:
  0.6 84.3 %shard_map.75 = (f32[64,512]{1,0:T(8,128)S(1)}, f32[32,64]{1,0:T(8,128)S(1)}, f32[32,8192]{1,0:T(8,128)S(1)}, f32[512,8192]{1,0:T(8,128)S(1)}, f32[256,8192]{1,0...) custom-call(f32[64,512]{1,0:T(8,128)} %bitcast.2, f32[32,64]{1,0:T(8,128)} %diag_ref.1, ...), custom_call_target="tpu_custom_call" | custom-call | tf_op jit(solution)/shard_map/pallas_call | solution.py:548
  85.0 6.3 %shard_map.76 = (f32[64,512]{1,0:T(8,128)}, f32[32,64]{1,0:T(8,128)}, f32[32,8192]{1,0:T(8,128)}, f32[512,8192]{1,0:T(8,128)}) custom-call(f32[64,512]{1,0:T(8,128)S(1)} %get-tuple-element.15.solved, f32[32,64]{1,0:T(8,128)S(1)} %get-tuple-element.16.inverse, f32[32,8192]{1,0:T(8,128)S(1)} %get-tuple-element.17.scaled, ...), custom_call_target="tpu_custom_call" | custom-call | tf_op jit(solution)/shard_map/pallas_call | solution.py:575

commit v5 on v4

--- a/solution.py
+++ b/solution.py
@@ -80,24 +80,27 @@
         pl.semaphore_signal(barrier, inc=1, device_id=at(mc_index, mr_index),
                             device_id_type=pl.DeviceIdType.MESH)
 
-    @pl.when(z > 0)
-    def _():
-        greet(down, mr)
+    pairs = n_mr // 2
+    y = mr // 2
+    core = lax.rem(mr, 2)
+
+    def tell(sem, mc_index, mr_index):
+        pl.semaphore_signal(ready_sem.at[sem], inc=1, device_id=at(mc_index, mr_index),
+                            device_id_type=pl.DeviceIdType.MESH)
 
     @pl.when(z < last)
     def _():
         greet(up, mr)
 
-    greet(across, mr)
-    twins = n_mr // 2 - 1 if n_mr % 2 == 0 else 0
-    if n_mr % 2 == 0:
-        greet(mc, mr + 1 - 2 * lax.rem(mr, 2))
-        for step in range(2, n_mr, 2):
-            greet(mc, lax.rem(mr + step, n_mr))
-    else:
-        for step in range(1, n_mr):
-            greet(mc, lax.rem(mr + step, n_mr))
-    greeted = 2 + twins if n_mr % 2 == 0 else n_mr
+    @pl.when(x == 0)
+    def _():
+        greet(across, mr)
+
+    greet(mc, mr + 1 - 2 * core)
+    for k in range(pairs):
+        @pl.when(k > y)
+        def _():
+            greet(mc, 2 * k + core)
 
     own_rows = pl.ds(pl.multiple_of(mc * rows, rows), rows)
     own_part = lambda k: pl.ds(pl.multiple_of(k * block_cols, block_cols), block_cols)
@@ -111,9 +114,20 @@
         own_rest = pltpu.make_async_copy(
             row_ref.at[:, pl.ds(width, cols - width)], panel.at[own_rows, pl.ds(width, cols - width)],
             load_sem.at[3])
-        own_rest.start()
-    own_column.start()
-    pl.semaphore_wait(barrier, greeted + jnp.where(z > 0, 1, 0) + jnp.where(z < last, 1, 0))
+    pl.semaphore_wait(barrier, 1 + y + x + jnp.where(z > 0, 1, 0))
+
+    @pl.when(z > 0)
+    def _():
+        tell(0, down, mr)
+
+    @pl.when(x == 1)
+    def _():
+        tell(1, across, mr)
+
+    for k in range(pairs - 1):
+        @pl.when(k < y)
+        def _():
+            tell(2, mc, 2 * k + core)
 
     def remote(ref, send, recv, mc_index, mr_index):
         return pltpu.make_async_remote_copy(
@@ -214,22 +228,54 @@
             else:
                 pl.when(sources[way])(functools.partial(act, way))
 
+    def open_way(way):
+        @pl.when(z < limit)
+        def _():
+            diag_line(z, way).start()
+
+        send = own_send.at[0] if final == 0 else None
+        (pair(mc, 0, send) if way == 2 else line(z, 0, way, send)).start()
+
     own_diag.wait()
-
-    @pl.when(z < limit)
-    def _():
-        each_side(lambda way: diag_line(z, way).start())
-
     own_first.wait()
-    send_row(0)
-    if twins:
-        for step in range(2, n_mr, 2):
-            pl.semaphore_signal(ready_sem.at[0], inc=1, device_id=at(mc, lax.rem(mr + step, n_mr)),
-                                device_id_type=pl.DeviceIdType.MESH)
+
+    @pl.when(z > 0)
+    def _():
+        open_way(0)
+
+    @pl.when(x == 1)
+    def _():
+        open_way(2)
+
+    if chunks > 1:
+        own_rest.start()
+    own_column.start()
+
+    @pl.when(x == 0)
+    def _():
+        pl.semaphore_wait(ready_sem.at[1], 1)
+        open_way(2)
+
+    @pl.when(z < last)
+    def _():
+        pl.semaphore_wait(ready_sem.at[0], 1)
+        open_way(1)
+
+    @pl.when(y < pairs - 1)
+    def _():
+        pl.semaphore_wait(ready_sem.at[2], pairs - 1 - y)
+
+    for k in range(1, pairs):
+        @pl.when(k > y)
+        def _():
+            tell(3, mc, 2 * k + core)
+
+    @pl.when(y > 0)
+    def _():
+        pl.semaphore_wait(ready_sem.at[3], y)
+
     if chunks > 1:
         own_rest.wait()
-    if twins:
-        pl.semaphore_wait(ready_sem.at[0], twins)
     if detour:
         @pl.when(mr == 0)
         def _():
@@ -566,7 +612,7 @@
             pltpu.VMEM((4, rows, max(detour, 128)), f32),
             dma((4,)), dma((1,)), dma((3,)), dma((max(1, levels - 1), chunks)), dma((2, chunks)), dma((chunks,)), dma((chunks,)),
             dma((3,)), dma((levels + 1,)), dma((1,)), dma((1,)), dma((1,)), dma((1,)),
-            dma((1,)), dma((2,)), dma((4,)), pltpu.SemaphoreType.REGULAR((1,)),
+            dma((1,)), dma((2,)), dma((4,)), pltpu.SemaphoreType.REGULAR((4,)),
         ],
         compiler_params=pltpu.CompilerParams(
             collective_id=0, has_side_effects=True, vmem_limit_bytes=VMEM_BYTES - held),

time: 91.4 us -> 91.2 us (level)
  no operation moved by 1% of the time
where the time goes in v5:
time: 91.2 us; the launch traced here: 91 us
  Pallas kernels  90.3 us (99%)
    pallas_call x1, Pallas kernels, shards(): pl.pallas_call(functools.partial(kernel, n_mc, n_mr, chunks, late, tile,...  84.1 us
    pallas_call x1, Pallas kernels, shards(): pl.pallas_call(functools.partial(finish, done, tile), out_shape=tuple((ja...  6.26 us

profile of v5, /device:TPU:0, one launch (start us, length us, event | category | flops | bytes accessed | tf_op | source)
XLA Modules:
  0.0 91.0 jit_solution(205361754416225317)
XLA Ops:
  0.6 84.1 %shard_map.75 = (f32[64,512]{1,0:T(8,128)S(1)}, f32[32,64]{1,0:T(8,128)S(1)}, f32[32,8192]{1,0:T(8,128)S(1)}, f32[512,8192]{1,0:T(8,128)S(1)}, f32[256,8192]{1,0...) custom-call(f32[64,512]{1,0:T(8,128)} %bitcast.2, f32[32,64]{1,0:T(8,128)} %diag_ref.1, ...), custom_call_target="tpu_custom_call" | custom-call | tf_op jit(solution)/shard_map/pallas_call | solution.py:594
  84.7 6.3 %shard_map.76 = (f32[64,512]{1,0:T(8,128)}, f32[32,64]{1,0:T(8,128)}, f32[32,8192]{1,0:T(8,128)}, f32[512,8192]{1,0:T(8,128)}) custom-call(f32[64,512]{1,0:T(8,128)S(1)} %get-tuple-element.15.solved, f32[32,64]{1,0:T(8,128)S(1)} %get-tuple-element.16.inverse, f32[32,8192]{1,0:T(8,128)S(1)} %get-tuple-element.17.scaled, ...), custom_call_target="tpu_custom_call" | custom-call | tf_op jit(solution)/shard_map/pallas_call | solution.py:621

commit v6 on v5

--- a/solution.py
+++ b/solution.py
@@ -169,27 +169,20 @@
         return remote(columns.at[own_part(k)], col_send.at[0], col_recv.at[0], mc, lax.rem(mr + step, n_mr))
 
     def send_row(c):
-        def send(span):
-            send = own_send.at[0] if c == final else None
-
-            @pl.when(z > 0)
-            def _():
-                line(z, c, 0, send, span).start()
-
-            @pl.when(z < last)
-            def _():
-                line(z, c, 1, send, span).start()
-
-            pair(mc, c, send, span).start()
-
-        if c == final and detour:
-            by_mr(lambda: send(kept), lambda: send(width))
-        else:
-            send(width)
-
-    def by_mr(first, others):
-        pl.when(mr == 0)(first)
-        pl.when(mr != 0)(others)
+        def make(way, send, span=None):
+            return pair(mc, c, send, span) if way == 2 else line(z, c, way, send, span)
+
+        def send(way):
+            if c != final:
+                make(way, None).start()
+            elif not detour or way == 1:
+                make(way, own_send.at[0]).start()
+            else:
+                trimmed = jnp.logical_and(mr == 0, x == (0 if way == 0 else 1))
+                pl.when(trimmed)(lambda: make(way, own_send.at[1], kept).start())
+                pl.when(jnp.logical_not(trimmed))(lambda: make(way, own_send.at[0]).start())
+
+        each_side(send)
 
     sides = (z > 0, z < last, None)
 
@@ -219,15 +212,6 @@
             src_ref=carried.at[1 + way], dst_ref=detoured(shard), send_sem=carry_send.at[1],
             recv_sem=carry_recv.at[1 + way], device_id=at(mc, 0), device_id_type=pl.DeviceIdType.MESH)
 
-    sources = (z < last, z > 0, None)
-
-    def each_source(act):
-        for way in range(3):
-            if sources[way] is None:
-                act(way)
-            else:
-                pl.when(sources[way])(functools.partial(act, way))
-
     def open_way(way):
         @pl.when(z < limit)
         def _():
@@ -314,7 +298,14 @@
             @pl.when(mr == n_mr - 1)
             def _():
                 carry_out().wait_recv()
-                each_side(lambda way: carry_on(way).start())
+
+                @pl.when(jnp.logical_and(z > 0, x == 0))
+                def _():
+                    carry_on(0).start()
+
+                @pl.when(x == 1)
+                def _():
+                    carry_on(2).start()
         if hop + 1 < chunks:
             send_row(hop + 1)
     for c in range(levels, chunks):
@@ -326,7 +317,13 @@
                 carry_on(way).wait_recv()
                 carry_home(way).start()
 
-            each_source(pass_home)
+            @pl.when(jnp.logical_and(z < last, x == 0))
+            def _():
+                pass_home(0)
+
+            @pl.when(x == 0)
+            def _():
+                pass_home(2)
 
     first_half_only = lambda q: jnp.logical_or(
         jnp.logical_and(q == last, z != last), jnp.logical_and(q == 0, z != 0))
@@ -433,7 +430,12 @@
                 make(kept).wait_recv()
                 carry_home(way).wait_recv()
 
-            by_mr(first, lambda: make(width).wait_recv())
+            if way == 1:
+                make(width).wait_recv()
+            else:
+                both = jnp.logical_and(mr == 0, x == 0)
+                pl.when(both)(first)
+                pl.when(jnp.logical_not(both))(lambda: make(width).wait_recv())
 
         split_last = phase == 0 and detour > 0
         pl.loop(0, chunks - 1 if split_last else chunks)(lambda c: step(c, whole))
@@ -482,9 +484,9 @@
         ref = panel.at[pl.ds(0, halves * half - rows // chunks)]
         remote(ref, send_sem.at[way], pair_recv.at[0], target[way], mr).wait_send()
 
-    def sent_own(count, span):
+    def sent_own(count, span, sem=0):
         ref = panel.at[pl.ds(0, count * rows), pl.ds(0, span)]
-        remote(ref, own_send.at[0], pair_recv.at[0], across, mr).wait_send()
+        remote(ref, own_send.at[sem], pair_recv.at[0], across, mr).wait_send()
 
     def sent_diag(way, count):
         if count > 0:
@@ -504,12 +506,25 @@
                 sent(1, 2 * (k + 1) + 1)
             sent(2, 2 * levels - (1 if k in (0, last) else 2))
             if detour:
-                by_mr(lambda: sent_own(count, kept), lambda: sent_own(count, width))
-
-                @pl.when(mr == n_mr - 1)
-                def _():
-                    sent_carry(0, count)
-                    sent_carry(1, count)
+                for side in range(2):
+                    trims = 1 if side == 1 or k > 0 else 0
+
+                    @pl.when(jnp.logical_and(mr == 0, x == side))
+                    def _():
+                        sent_own(count - trims, width)
+                        if trims:
+                            sent_own(trims, kept, 1)
+
+                    @pl.when(jnp.logical_and(mr == n_mr - 1, x == side))
+                    def _():
+                        if trims:
+                            sent_carry(0, trims)
+                        if side == 0:
+                            sent_carry(1, 1 + (k < last))
+
+                @pl.when(mr != 0)
+                def _():
+                    sent_own(count, width)
             else:
                 sent_own(count, width)
             for m in range(n_mr):
@@ -612,7 +627,7 @@
             pltpu.VMEM((4, rows, max(detour, 128)), f32),
             dma((4,)), dma((1,)), dma((3,)), dma((max(1, levels - 1), chunks)), dma((2, chunks)), dma((chunks,)), dma((chunks,)),
             dma((3,)), dma((levels + 1,)), dma((1,)), dma((1,)), dma((1,)), dma((1,)),
-            dma((1,)), dma((2,)), dma((4,)), pltpu.SemaphoreType.REGULAR((4,)),
+            dma((2,)), dma((2,)), dma((4,)), pltpu.SemaphoreType.REGULAR((4,)),
         ],
         compiler_params=pltpu.CompilerParams(
             collective_id=0, has_side_effects=True, vmem_limit_bytes=VMEM_BYTES - held),

time: 91.2 us -> 91.2 us (level)
  no operation moved by 1% of the time
where the time goes in v6:
time: 91.2 us; the launch traced here: 91 us
  Pallas kernels  90.3 us (99%)
    pallas_call x1, Pallas kernels, shards(): pl.pallas_call(functools.partial(kernel, n_mc, n_mr, chunks, late, tile,...  84.1 us
    pallas_call x1, Pallas kernels, shards(): pl.pallas_call(functools.partial(finish, done, tile), out_shape=tuple((ja...  6.26 us

profile of v6, /device:TPU:0, one launch (start us, length us, event | category | flops | bytes accessed | tf_op | source)
XLA Modules:
  0.0 91.0 jit_solution(10151398366545581086)
XLA Ops:
  0.6 84.1 %shard_map.75 = (f32[64,512]{1,0:T(8,128)S(1)}, f32[32,64]{1,0:T(8,128)S(1)}, f32[32,8192]{1,0:T(8,128)S(1)}, f32[512,8192]{1,0:T(8,128)S(1)}, f32[256,8192]{1,0...) custom-call(f32[64,512]{1,0:T(8,128)} %bitcast.2, f32[32,64]{1,0:T(8,128)} %diag_ref.1, ...), custom_call_target="tpu_custom_call" | custom-call | tf_op jit(solution)/shard_map/pallas_call | solution.py:609
  84.7 6.3 %shard_map.76 = (f32[64,512]{1,0:T(8,128)}, f32[32,64]{1,0:T(8,128)}, f32[32,8192]{1,0:T(8,128)}, f32[512,8192]{1,0:T(8,128)}) custom-call(f32[64,512]{1,0:T(8,128)S(1)} %get-tuple-element.15.solved, f32[32,64]{1,0:T(8,128)S(1)} %get-tuple-element.16.inverse, f32[32,8192]{1,0:T(8,128)S(1)} %get-tuple-element.17.scaled, ...), custom_call_target="tpu_custom_call" | custom-call | tf_op jit(solution)/shard_map/pallas_call | solution.py:636
